TPU v7x, 32 devices: a whole 2x2x4 slice. The times are simulated.
32 devices in a mesh: prow: 16 (over z, y, core), pcol: 2 (over x).
Axes of the slice: x: 2, y: 2, z: 4, core: 2. Of those that a mesh axis runs over, the one named last changes fastest.
Arguments:
- factor_panel: float32 [2048, 31744], P('pcol', 'prow'), may hold values from -0.03125 to 0.03125
- whitened_before: float32 [31744, 4096], P('prow', 'pcol'), may hold values from -6 to 6
- green_panel: float32 [2048, 4096], P('prow', 'pcol'), may hold values from -6 to 6
- diag_inverse: float32 [2048, 2048], P('prow', 'pcol'), may hold values from -1 to 8, as said below
Outputs:
- whitened: float32 [2048, 4096], P('prow', 'pcol')
- gram_block: float32 [4096, 4096], P('prow', 'pcol')
Inputs may be any that keep to these rules, and one draw needn't show every extreme that they name: `diag_inverse`: zero above the diagonal and positive on it.
All inputs are finite; a program needn't handle non-finite values.
Results may differ from a plain program's by a relative error of at most 0.00012.
Values sent between devices are 32-bit elements; how exact they have to be, the bound alone decides.
No kernel may reach another device: no remote copies, remote signals or barrier semaphores. Data moves between devices by JAX's collectives and lax.ppermute only.
A program may use at most 128 MiB of HBM per device.

v0:
```python
import jax
import jax.numpy as jnp
from jax import lax
from jax.sharding import PartitionSpec as P

P_SIZE = 4096
B = 2048


highest = lax.Precision.HIGHEST


def from_root(value, axis, source):
    kept = jnp.where(lax.axis_index(axis) == source, value, 0).astype(value.dtype)
    return lax.psum(kept, axis)


def shards(factor_panel, whitened_before, green_panel, diag_inverse):
    rows_all = lax.all_gather(factor_panel, "pcol", axis=0, tiled=True)
    update = lax.psum_scatter(
        jnp.dot(rows_all, whitened_before, precision=highest, preferred_element_type=jnp.float32),
        "prow",
        scatter_dimension=0,
        tiled=True,
    )
    own_rows = green_panel - update
    remaining = lax.all_gather(own_rows, "prow", axis=0, tiled=True)
    whitened = jnp.dot(
        lax.all_gather(diag_inverse, "pcol", axis=1, tiled=True),
        remaining,
        precision=highest,
        preferred_element_type=jnp.float32,
    )
    contract = (((0,), (0,)), ((), ()))
    column_all = lax.all_gather(whitened, "prow", axis=0, tiled=True)
    sub_width = P_SIZE // lax.axis_size("prow")
    local_width = P_SIZE // lax.axis_size("pcol")
    row_index = lax.axis_index("prow")
    root_col = row_index * lax.axis_size("pcol") // lax.axis_size("prow")
    offset_cols = row_index * sub_width % local_width
    own_block = lax.dynamic_slice_in_dim(column_all, offset_cols, sub_width, 1)
    needed = from_root(own_block, "pcol", root_col)
    gram_block = lax.dot_general(
        needed, column_all, contract, precision=highest, preferred_element_type=jnp.float32
    ) * (1.0 / B)
    return (whitened, gram_block)


def solution(mesh):
    return jax.shard_map(
        shards,
        mesh=mesh,
        in_specs=(P("pcol", "prow"), P("prow", "pcol"), P("prow", "pcol"), P("prow", "pcol")),
        out_specs=(P("prow", "pcol"), P("prow", "pcol")),
        check_vma=False,
    )
```

profile of v0, /device:TPU:0, one launch (start us, length us, event | category | flops | bytes accessed | tf_op | source)
XLA Modules:
  0.0 895.3 jit_solution(7894352029425034349)
XLA Ops:
  7.2 0.0 all-gather.5.cloned.1.call-start
  7.2 0.7 all-gather.5.cloned.1.call-update
  7.9 0.0 reduce-scatter.2.cloned.1.call-start
  7.9 197.3 %all-gather.5.cloned.1.call-done = f32[2048,1984]{0,1:T(8,128)} async-done(((f32[1024,1984]{0,1:T(8,128)}), f32[2048,1984]{0,1:T(8,128)}) %all-gather.5.cloned.1.call-update) | async-done | bytes 16252944 | tf_op jit(solution)/shard_map/all_gather | solution.py:19
  205.2 113.6 %fusion = f32[2048,2048]{1,0:T(8,128)} fusion(f32[2048,1984]{0,1:T(8,128)} %all-gather.5.cloned.1.call-done, f32[1984,2048]{1,0:T(8,128)} %param.5), kind=kOutput, calls=%fused_computation.3 | convolution fusion | flops 99857989632 | bytes 49283072 | tf_op jit(solution)/shard_map/dot_general | solution.py:21
  318.8 0.0 reduce-scatter.2.cloned.1.call-update
  318.9 0.0 all-gather.9.cloned.1.call-start
  318.9 0.7 all-gather.9.cloned.1.call-update
  319.6 0.0 all-gather.7.cloned.1.call-start
  319.7 176.7 %reduce-scatter.2.cloned.1.call-done = f32[128,2048]{1,0:T(8,128)} async-done(((f32[2048,2048]{1,0:T(8,128)}), f32[128,2048]{1,0:T(8,128)}) %reduce-scatter.2.cloned.1.call-update) | async-done | bytes 1048592 | tf_op jit(solution)/shard_map/reduce_scatter | solution.py:20
  496.4 2.3 sub.7
  498.7 0.0 all-gather.7.cloned.1.call-update
  498.7 0.2 all-gather.11.cloned.1.call-start
  498.9 19.4 %all-gather.9.cloned.1.call-done = f32[128,2048]{1,0:T(8,128)} async-done(((f32[128,1024]{1,0:T(8,128)}), f32[128,2048]{1,0:T(8,128)}) %all-gather.9.cloned.1.call-update) | async-done | bytes 1048592 | tf_op jit(solution)/shard_map/all_gather | solution.py:29
  518.3 129.1 %all-gather.7.cloned.1.call-done = f32[2048,2048]{1,0:T(8,128)} async-done(((f32[128,2048]{1,0:T(8,128)}), f32[2048,2048]{1,0:T(8,128)}) %all-gather.7.cloned.1.call-update) | async-done | bytes 16777232 | tf_op jit(solution)/shard_map/all_gather | solution.py:27
  647.4 29.9 %convolution_bitcast_fusion = f32[128,2048]{0,1:T(8,128)} fusion(f32[2048,2048]{1,0:T(8,128)} %all-gather.7.cloned.1.call-done, f32[128,2048]{1,0:T(8,128)} %all-gather.9.cloned.1.call-done), kind=kOutput, calls=%fused_computation.1 | convolution fusion | flops 6442450944 | bytes 18874368 | tf_op jit(solution)/shard_map/dot_general | solution.py:28
  677.3 0.0 all-gather.11.cloned.1.call-update
  677.3 0.0 all-reduce.2.cloned.1.call-start
  677.4 128.1 %all-gather.11.cloned.1.call-done = f32[2048,2048]{0,1:T(8,128)} async-done(((f32[128,2048]{0,1:T(8,128)}), f32[2048,2048]{0,1:T(8,128)}) %all-gather.11.cloned.1.call-update) | async-done | bytes 16777232 | tf_op jit(solution)/shard_map/all_gather | solution.py:35
  805.5 3.1 dynamic-slice_select_fusion
  808.6 0.0 all-reduce.2.cloned.1.call-update
  808.7 2.5 copy.6
  811.2 58.8 %all-reduce.2.cloned.1.call-done = f32[2048,256]{0,1:T(8,128)} async-done(((f32[2048,256]{0,1:T(8,128)}), f32[2048,256]{0,1:T(8,128)}) %all-reduce.2.cloned.1.call-update) | async-done | bytes 2097168 | tf_op jit(solution)/shard_map/psum | solution.py:15
  870.0 18.5 %convolution_multiply_fusion = f32[256,2048]{1,0:T(8,128)} fusion(f32[2048,256]{0,1:T(8,128)} %all-reduce.2.cloned.1.call-done, f32[2048,2048]{0,1:T(8,128)} %all-gather.11.cloned.1.call-done), kind=kOutput, calls=%fused_computation | convolution fusion | flops 12885426176 | bytes 20971520 | tf_op jit(solution)/shard_map/dot_general | solution.py:43
  (2 shorter events, 0.0 us)
Async XLA Ops:
  7.2 198.1 %all-gather.5.cloned.1.call-start = ((), (), s32[]{:S(2)}) async-start(), calls=%async_computation.1 | async-start | bytes 24379392 | tf_op jit(solution)/shard_map/all_gather | solution.py:19
  7.9 488.5 %reduce-scatter.2.cloned.1.call-start = ((), (), s32[]{:S(2)}) async-start(), calls=%async_computation.2 | async-start | bytes 17825792 | tf_op jit(solution)/shard_map/reduce_scatter | solution.py:20
  318.8 177.5 %copy-start = (f32[128,2048]{1,0:T(8,128)S(1)}, f32[128,2048]{1,0:T(8,128)}, u32[]{:S(2)}) copy-start(f32[128,2048]{1,0:T(8,128)} %param.6) | copy-start | bytes 3145732
  318.9 199.5 %all-gather.9.cloned.1.call-start = ((), (), s32[]{:S(2)}) async-start(), calls=%async_computation.4 | async-start | bytes 1572864 | tf_op jit(solution)/shard_map/all_gather | solution.py:29
  319.6 327.8 %all-gather.7.cloned.1.call-start = ((), (), s32[]{:S(2)}) async-start(), calls=%async_computation.3 | async-start | bytes 17825792 | tf_op jit(solution)/shard_map/all_gather | solution.py:27
  498.7 306.8 %all-gather.11.cloned.1.call-start = ((), (), s32[]{:S(2)}) async-start(), calls=%async_computation.5 | async-start | bytes 17825792 | tf_op jit(solution)/shard_map/all_gather | solution.py:35
  677.3 192.7 %all-reduce.2.cloned.1.call-start = ((), (), s32[]{:S(2)}) async-start(), calls=%async_computation.6 | async-start | bytes 4194304 | tf_op jit(solution)/shard_map/psum | solution.py:15
Sparse Core Ops, SparseCore 0:
  9.5 195.6 all-gather.4
  319.0 177.3 reduce-scatter.1
  497.9 20.3 all-gather.8
  520.9 126.4 all-gather.6
  677.4 128.0 all-gather.10
  808.8 61.1 all-reduce.1
where the time goes:
time: 896 us; the launch traced here: 895 us
  waiting for transfers between devices  711 us (79%)
  matrix products  162 us (18%)
  between operations  14.1 us (2%)
    all_gather x1, waiting for transfers between devices, shards(): rows_all = lax.all_gather(factor_panel, 'pcol', axis=0, tiled=True)  197 us
    reduce_scatter x1, waiting for transfers between devices, shards(): lax.psum_scatter(jnp.dot(rows_all, whitened_before, precision=highest, pr...  177 us
    all_gather x1, waiting for transfers between devices, shards(): remaining = lax.all_gather(own_rows, 'prow', axis=0, tiled=True)  129 us
    all_gather x1, waiting for transfers between devices, shards(): column_all = lax.all_gather(whitened, 'prow', axis=0, tiled=True)  128 us
    dot_general x1, matrix products, shards(): jnp.dot(rows_all, whitened_before, precision=highest, preferred_element_t...  114 us
    psum x1, waiting for transfers between devices, from_root(): return lax.psum(kept, axis)  58.8 us
    dot_general x1, matrix products, shards(): jnp.dot(lax.all_gather(diag_inverse, 'pcol', axis=1, tiled=True), remaini...  29.9 us
    all_gather x1, waiting for transfers between devices, shards(): lax.all_gather(diag_inverse, 'pcol', axis=1, tiled=True)  19.4 us
  transfers between devices with their start and end apart: 6, of which 6 were waited for; matrix products, arithmetic and copies ran while one was open for 1% of the time, Pallas kernels for 0%

commit v1 on v0

v1 whole, which is shorter than its diff:
```python
import jax
import jax.numpy as jnp
from jax import lax
from jax.sharding import PartitionSpec as P


OWN_PARTS = (1, 3)
RECV_PARTS = (3, 3, 2)
TAIL_PARTS = (1, 1)

high = lax.Precision.HIGH


def mm(a, b):
    return jnp.dot(a, b, precision=high, preferred_element_type=jnp.float32)


def mm_t(a, b):
    return lax.dot_general(a, b, (((0,), (0,)), ((), ())), precision=high, preferred_element_type=jnp.float32)


def spans(parts, total):
    unit = total // sum(parts)
    out, at = [], 0
    for p in parts:
        out.append((at, at + p * unit))
        at += p * unit
    return out


def gather_rows(value, r, bits, size):
    done = []
    for bit in bits:
        got = lax.ppermute(value, "prow", [(i, i ^ bit) for i in range(size)])
        mine = (r & bit) != 0
        axis = sum(1 for b in done if b > bit)
        value = jnp.stack([jnp.where(mine, got, value), jnp.where(mine, value, got)], axis=axis)
        done.append(bit)
    return value.reshape((-1, value.shape[-1]))


def bit_list(size):
    return [1 << k for k in range(size.bit_length() - 1)]


def swap(value, bit, size):
    return lax.ppermute(value, "prow", [(i, i ^ bit) for i in range(size)])


def scatter_columns(value, r, size):
    for bit in bit_list(size):
        w = value.shape[1] // 2
        mine = (r & bit) != 0
        left, right = value[:, :w], value[:, w:]
        got = swap(jnp.where(mine, left, right), bit, size)
        value = jnp.where(mine, right, left) + got
    return value


def gather_columns(value, r, size):
    held = None
    for bit in reversed(bit_list(size)):
        got = swap(value, bit, size)
        if bit == 1:
            return held, value, got
        mine = (r & bit) != 0
        value = jnp.concatenate([jnp.where(mine, got, value), jnp.where(mine, value, got)], axis=1)
        held = value if held is None else held


def column_slot(r, size):
    n = len(bit_list(size))
    return sum(((r >> k) & 1) << (n - 1 - k) for k in range(n))


def pair_shards(factor, before, green, dinv):
    size = lax.axis_size("prow")
    r = lax.axis_index("prow")
    c = lax.axis_index("pcol")
    first = c == 0
    half, rows_g = factor.shape[0], green.shape[0]
    width = before.shape[1]
    panel = 2 * half
    top = size // 2
    cross = [(0, 1), (1, 0)]
    own_spans = spans(OWN_PARTS, half)
    recv_spans = spans(RECV_PARTS, half)

    came = []
    for lo, hi in recv_spans:
        came.append(lax.ppermute(factor[lo:hi], "pcol", cross))

    def reduced(rows, base):
        n = rows.shape[0] // rows_g
        prod, placed = lax.optimization_barrier((mm(rows, before), green))
        prod = prod.reshape(n, rows_g, width)
        here = (base // rows_g + lax.broadcasted_iota(jnp.int32, (n, 1, 1), 0)) == r
        part = (jnp.where(here, placed[None], 0.0) - prod).reshape(n * rows_g, width)
        return scatter_columns(part, r, size)

    rem_own = jnp.concatenate([reduced(factor[lo:hi], c * half + lo) for lo, hi in own_spans], axis=0)

    other = lax.ppermute(dinv, "pcol", cross)
    dleft = jnp.where(first, dinv, other)
    dright = jnp.where(first, other, dinv)
    bits = bit_list(size)
    got = lax.ppermute(dright, "prow", [(i, i - top) for i in range(top, size)])
    dright = jnp.where(r >= top, dright, got)
    dleft = gather_rows(dleft, r, bits[::-1], size)
    dright = gather_rows(dright, r, bits[1:-1] + bits[:1], size)

    pairs = []
    for cn in (0, 1):
        for i in range(cn * top, (cn + 1) * top):
            pairs.append((i * 2 + cn, (cn * top + column_slot(i, size) // 2) * 2 + 1 - cn))

    def finish(x):
        held, kept, got = gather_columns(x, r, size)
        crossed = lax.ppermute(held, ("prow", "pcol"), pairs)
        return kept, got, crossed

    rem_recv, recv_done = [], []
    for rows, (lo, hi) in zip(came, recv_spans):
        rem_recv.append(reduced(rows, (1 - c) * half + lo))
        known = jnp.concatenate(rem_recv, axis=0)
        by_own = jnp.where(first, dleft[half + lo:half + hi], 0.0)
        by_recv = jnp.where(first, dright[lo:hi, :hi], dleft[lo:hi, :hi])
        x = mm(by_own, rem_own) + mm(by_recv, known)
        recv_done.append(finish(x))
    by_own = jnp.where(first, dleft[:half], dright)
    by_recv = jnp.where(first, 0.0, dleft[half:])
    x_own = mm(by_own, rem_own) + mm(by_recv, known)
    cut = lax.optimization_barrier([x_own[lo:hi] for lo, hi in spans(TAIL_PARTS, half)])
    own_done = [finish(x) for x in cut]
    cross_recv = jnp.concatenate([v[2] for v in recv_done], axis=0)
    cross_own = jnp.concatenate([v[2] for v in own_done], axis=0)

    sub = 2 * width // size
    wide = width // 2
    upper = (r >= top) == (c == 1)
    odd = (r & 1) != 0
    start = (r % top) * sub
    in_kept = (start >= wide) == odd
    at = (r % top) * rows_g
    grams = [jnp.zeros((sub, wide), jnp.float32)] * 2
    rows_kept, rows_got = jnp.zeros((rows_g, wide), jnp.float32), jnp.zeros((rows_g, wide), jnp.float32)
    groups = [(recv_done, recv_spans, cross_own, ~upper), (own_done, spans(TAIL_PARTS, half), cross_recv, upper)]
    for done, cuts, cross_all, holds in groups:
        for (kept, got, _), (lo, hi) in zip(done, cuts):
            pieces = [lax.dynamic_slice_in_dim(v, start % wide, sub, 1) for v in (kept, got)]
            needed = jnp.where(upper, jnp.where(in_kept, *pieces), cross_all[lo:hi])
            grams = [g + mm_t(needed, v) for g, v in zip(grams, (kept, got))]
            hit = holds & (at >= lo) & (at < hi)
            spot = jnp.clip(at - lo, 0, hi - lo - rows_g)
            rows_kept = jnp.where(hit, lax.dynamic_slice_in_dim(kept, spot, rows_g, 0), rows_kept)
            rows_got = jnp.where(hit, lax.dynamic_slice_in_dim(got, spot, rows_g, 0), rows_got)

    def ordered(kept, got):
        return jnp.concatenate([jnp.where(odd, got, kept), jnp.where(odd, kept, got)], axis=1)

    return ordered(rows_kept, rows_got), ordered(*grams) * (1.0 / panel)


def many_shards(factor, before, green, dinv):
    rows_all = lax.all_gather(factor, "pcol", axis=0, tiled=True)
    update = lax.psum_scatter(mm(rows_all, before), "prow", scatter_dimension=0, tiled=True)
    remaining = lax.all_gather(green - update, "prow", axis=0, tiled=True)
    whitened = mm(lax.all_gather(dinv, "pcol", axis=1, tiled=True), remaining)
    column_all = lax.all_gather(whitened, "prow", axis=0, tiled=True)
    rows, cols = lax.axis_size("prow"), lax.axis_size("pcol")
    local_width = before.shape[1]
    sub_width = local_width * cols // rows
    row = lax.axis_index("prow")
    own = lax.dynamic_slice_in_dim(column_all, row * sub_width % local_width, sub_width, 1)
    kept = jnp.where(lax.axis_index("pcol") == row * cols // rows, own, 0.0)
    gram = mm_t(lax.psum(kept, "pcol"), column_all) * (1.0 / column_all.shape[0])
    return whitened, gram


def solution(mesh):
    rows, cols = mesh.shape["prow"], mesh.shape["pcol"]
    paired = cols == 2 and rows & (rows - 1) == 0 and rows == 16

    def body(*args):
        if not paired:
            return many_shards(*args)
        return pair_shards(*args)

    return jax.shard_map(
        body,
        mesh=mesh,
        in_specs=(P("pcol", "prow"), P("prow", "pcol"), P("prow", "pcol"), P("prow", "pcol")),
        out_specs=(P("prow", "pcol"), P("prow", "pcol")),
        check_vma=False,
    )
```

time: 896 us -> 598 us (0.67); the launches traced: 895 us -> 588 us
  waiting for transfers between devices: 711 us -> 324 us
  other arithmetic: 5.44 us -> 71.5 us
  starting transfers between devices: 0.42 us -> 63.7 us
  matrix products: 162 us -> 112 us
  local copies, waits for them, and re-layouts: 2.54 us -> 14.6 us
  between operations: 14.1 us -> 2.45 us
    all_gather x4 -> x0, waiting for transfers between devices: 474 us -> none  [the longest x1 197 us: shards(): rows_all = lax.all_gather(factor_panel, 'pcol', axis=0, tiled=True)]
    ppermute x0 -> x57, waiting for transfers between devices: none -> 324 us  [the longest x40 241 us: swap(): return lax.ppermute(value, 'prow', [(i, i ^ bit) for i in range(size)])]
    reduce_scatter x1 -> x0, waiting for transfers between devices: 177 us -> none  [shards(): lax.psum_scatter(jnp.dot(rows_all, whitened_before, precision=highest, pr...]
    ppermute x0 -> x57, starting transfers between devices: none -> 63.7 us  [the longest x40 23.8 us: swap(): return lax.ppermute(value, 'prow', [(i, i ^ bit) for i in range(size)])]
    psum x1 -> x0, waiting for transfers between devices: 58.8 us -> none  [from_root(): return lax.psum(kept, axis)]
    dot_general x3 -> x23, matrix products: 162 us -> 112 us  [the longest x13 94.1 us: mm(): return jnp.dot(a, b, precision=high, preferred_element_type=jnp.float32)]
    another operation x0 -> x15, other arithmetic: none -> 18.7 us  [gather_rows(): jnp.stack([jnp.where(mine, got, value), jnp.where(mine, value, got)], axi...]
    select_n x1 -> x43, other arithmetic: 3.13 us -> 19.3 us  [the longest x20 8.34 us: scatter_columns(): got = swap(jnp.where(mine, left, right), bit, size)]
  transfers between devices with their start and end apart: 6 -> 57, of which waited for: 6 -> 34; matrix products, arithmetic and copies ran while one was open for 1% -> 27% of each run, Pallas kernels for 0% -> 0%
where the time goes in v1:
time: 598 us; the launch traced here: 588 us
  waiting for transfers between devices  324 us (54%)
  matrix products  112 us (19%)
  other arithmetic  71.5 us (12%)
  starting transfers between devices  63.7 us (11%)
  local copies, waits for them, and re-layouts  14.6 us (2%)
    ppermute x40, waiting for transfers between devices, swap(): return lax.ppermute(value, 'prow', [(i, i ^ bit) for i in range(size)])  241 us
    dot_general x13, matrix products, mm(): return jnp.dot(a, b, precision=high, preferred_element_type=jnp.float32)  94.1 us
    ppermute x7, waiting for transfers between devices, gather_rows(): got = lax.ppermute(value, 'prow', [(i, i ^ bit) for i in range(size)])  40.7 us
    ppermute x40, starting transfers between devices, swap(): return lax.ppermute(value, 'prow', [(i, i ^ bit) for i in range(size)])  23.8 us
    ppermute x1, waiting for transfers between devices, pair_shards(): got = lax.ppermute(dright, 'prow', [(i, i - top) for i in range(top, size)])  23.1 us
    ppermute x5, waiting for transfers between devices, finish(): crossed = lax.ppermute(held, ('prow', 'pcol'), pairs)  19.3 us
    another operation x15, other arithmetic, gather_rows(): jnp.stack([jnp.where(mine, got, value), jnp.where(mine, value, got)], axi...  18.7 us
    dot_general x10, matrix products, mm_t(): lax.dot_general(a, b, (((0,), (0,)), ((), ())), precision=high, preferred...  17.9 us
  transfers between devices with their start and end apart: 57, of which 34 were waited for; matrix products, arithmetic and copies ran while one was open for 27% of the time, Pallas kernels for 0%

profile of v1, /device:TPU:0, one launch (start us, length us, event | category | flops | bytes accessed | tf_op | source)
XLA Modules:
  0.0 588.0 jit_solution(3094181324784419198)
XLA Ops:
  6.8 11.4 %fusion.10 = f32[256,2048]{1,0:T(8,128)S(1)} fusion(f32[1984,2048]{1,0:T(8,128)} %param.5, f32[1024,1984]{0,1:T(8,128)} %param.4), kind=kOutput, calls=%fused_computation.54 | convolution fusion | flops 6241124352 | bytes 20381696 | tf_op jit(solution)/shard_map/dot_general | solution.py:15
  27.0 25.9 %fusion.1 = f32[768,2048]{1,0:T(8,128)} fusion(f32[1984,2048]{1,0:T(8,128)} %param.5, f32[1024,1984]{0,1:T(8,128)} %param.4), kind=kOutput, calls=%fused_computation.7 | convolution fusion | flops 18723373056 | bytes 28639232 | tf_op jit(solution)/shard_map/dot_general | solution.py:15
  61.0 11.1 %collective-permute-start.5 = (f32[128,1024]{1,0:T(8,128)S(1)}, f32[128,1024]{1,0:T(8,128)S(1)}, u32[]{:S(2)}, u32[]{:S(2)}) collective-permute-start(f32[128,1024]{1,0:T(8,128)S(1)} %get-tuple-element.61), channel_id=1, source_target_pairs={{16,0},{18,2},{20,4},{22,6},{24,8},{26,10},{28,12},{30,14},{17,1},... | collective-permute-start | bytes 1572872 | tf_op jit(solution)/shard_map/ppermute | solution.py:107
  77.3 23.1 %collective-permute-done.5 = f32[128,1024]{1,0:T(8,128)S(1)} collective-permute-done((f32[128,1024]{1,0:T(8,128)S(1)}, f32[128,1024]{1,0:T(8,128)S(1)}, u32[]{:S(2)}, u32[]{:S(2)}) %collective-permute-start.5) | collective-permute-done | bytes 524320 | tf_op jit(solution)/shard_map/ppermute | solution.py:107
  102.0 8.3 %collective-permute-done.1 = f32[128,1024]{1,0:T(8,128)S(1)} collective-permute-done((f32[128,1024]{1,0:T(8,128)S(1)}, f32[128,1024]{1,0:T(8,128)S(1)}, u32[]{:S(2)}, u32[]{:S(2)}) %collective-permute-start.1) | collective-permute-done | bytes 524320 | tf_op jit(solution)/shard_map/ppermute | solution.py:34
  113.6 9.6 %collective-permute-done.6 = f32[128,1024]{1,0:T(8,128)S(1)} collective-permute-done((f32[128,1024]{1,0:T(8,128)S(1)}, f32[128,1024]{1,0:T(8,128)S(1)}, u32[]{:S(2)}, u32[]{:S(2)}) %collective-permute-start.6) | collective-permute-done | bytes 524320 | tf_op jit(solution)/shard_map/ppermute | solution.py:34
  139.6 12.8 %fusion.85 = f32[256,2048]{1,0:T(8,128)} fusion(f32[256,1984]{0,1:T(8,128)} %collective-permute-done.27, f32[1984,2048]{1,0:T(8,128)S(1)} %bitcast.97), kind=kOutput, calls=%fused_computation.255 | convolution fusion | flops 6241124352 | bytes 20381696 | tf_op jit(solution)/shard_map/dot_general | solution.py:15
  155.5 7.7 %collective-permute-done.2 = f32[2,128,1024]{2,1,0:T(8,128)} collective-permute-done((f32[2,128,1024]{2,1,0:T(8,128)}, f32[2,128,1024]{2,1,0:T(8,128)}, u32[]{:S(2)}, u32[]{:S(2)}) %collective-permute-start.2) | collective-permute-done | bytes 1048608 | tf_op jit(solution)/shard_map/ppermute | solution.py:34
  166.7 15.1 %collective-permute-done.7 = f32[2,128,1024]{2,1,0:T(8,128)} collective-permute-done((f32[2,128,1024]{2,1,0:T(8,128)}, f32[2,128,1024]{2,1,0:T(8,128)}, u32[]{:S(2)}, u32[]{:S(2)}) %collective-permute-start.7) | collective-permute-done | bytes 1048608 | tf_op jit(solution)/shard_map/ppermute | solution.py:34
  187.1 18.1 %fusion.84 = f32[384,2048]{1,0:T(8,128)} fusion(f32[384,1984]{0,1:T(8,128)} %collective-permute-done.22, f32[1984,2048]{1,0:T(8,128)S(1)} %bitcast.97), kind=kOutput, calls=%fused_computation.254 | convolution fusion | flops 9361686528 | bytes 22446080 | tf_op jit(solution)/shard_map/dot_general | solution.py:15
  214.6 18.5 %fusion.83 = f32[384,2048]{1,0:T(8,128)} fusion(f32[384,1984]{0,1:T(8,128)} %collective-permute-done.17, f32[1984,2048]{1,0:T(8,128)S(1)} %bitcast.97), kind=kOutput, calls=%fused_computation.253 | convolution fusion | flops 9361686528 | bytes 22446080 | tf_op jit(solution)/shard_map/dot_general | solution.py:15
  247.8 8.4 %collective-permute-done.31 = f32[256,128]{1,0:T(8,128)S(1)} collective-permute-done((f32[256,128]{1,0:T(8,128)S(1)}, f32[256,128]{1,0:T(8,128)S(1)}, u32[]{:S(2)}, u32[]{:S(2)}) %collective-permute-start.31) | collective-permute-done | bytes 131104 | tf_op jit(solution)/shard_map/ppermute | solution.py:47
  270.0 23.4 %collective-permute-done.14 = f32[768,512]{1,0:T(8,128)S(1)} collective-permute-done((f32[768,512]{1,0:T(8,128)S(1)}, f32[768,512]{1,0:T(8,128)S(1)}, u32[]{:S(2)}, u32[]{:S(2)}) %collective-permute-start.14) | collective-permute-done | bytes 1572896 | tf_op jit(solution)/shard_map/ppermute | solution.py:47
  294.2 16.1 %collective-permute-done.24 = f32[384,512]{1,0:T(8,128)S(1)} collective-permute-done((f32[384,512]{1,0:T(8,128)S(1)}, f32[384,512]{1,0:T(8,128)S(1)}, u32[]{:S(2)}, u32[]{:S(2)}) %collective-permute-start.24) | collective-permute-done | bytes 786464 | tf_op jit(solution)/shard_map/ppermute | solution.py:47
  310.7 15.5 %collective-permute-done.19 = f32[384,512]{1,0:T(8,128)S(1)} collective-permute-done((f32[384,512]{1,0:T(8,128)S(1)}, f32[384,512]{1,0:T(8,128)S(1)}, u32[]{:S(2)}, u32[]{:S(2)}) %collective-permute-start.19) | collective-permute-done | bytes 786464 | tf_op jit(solution)/shard_map/ppermute | solution.py:47
  330.0 13.0 %collective-permute-done.20 = f32[384,256]{1,0:T(8,128)S(1)} collective-permute-done((f32[384,256]{1,0:T(8,128)S(1)}, f32[384,256]{1,0:T(8,128)S(1)}, u32[]{:S(2)}, u32[]{:S(2)}) %collective-permute-start.20) | collective-permute-done | bytes 393248 | tf_op jit(solution)/shard_map/ppermute | solution.py:47
  343.2 13.4 %collective-permute-done.16 = f32[768,128]{1,0:T(8,128)S(1)} collective-permute-done((f32[768,128]{1,0:T(8,128)S(1)}, f32[768,128]{1,0:T(8,128)S(1)}, u32[]{:S(2)}, u32[]{:S(2)}) %collective-permute-start.16) | collective-permute-done | bytes 393248 | tf_op jit(solution)/shard_map/ppermute | solution.py:47
  382.6 19.1 %collective-permute-done.40 = f32[256,128]{1,0:T(8,128)S(1)} collective-permute-done((f32[256,128]{1,0:T(8,128)S(1)}, f32[256,128]{1,0:T(8,128)S(1)}, u32[]{:S(2)}, u32[]{:S(2)}) %collective-permute-start.40) | collective-permute-done | bytes 131104 | tf_op jit(solution)/shard_map/ppermute | solution.py:47
  426.1 8.3 %collective-permute-done.45 = f32[384,256]{1,0:T(8,128)S(1)} collective-permute-done((f32[384,256]{1,0:T(8,128)S(1)}, f32[384,256]{1,0:T(8,128)S(1)}, u32[]{:S(2)}, u32[]{:S(2)}) %collective-permute-start.45) | collective-permute-done | bytes 393248 | tf_op jit(solution)/shard_map/ppermute | solution.py:47
  444.8 20.5 %collective-permute-done.33 = f32[512,256]{1,0:T(8,128)S(1)} collective-permute-done((f32[512,256]{1,0:T(8,128)S(1)}, f32[512,256]{1,0:T(8,128)S(1)}, u32[]{:S(2)}, u32[]{:S(2)}) %collective-permute-start.33) | collective-permute-done | bytes 524320 | tf_op jit(solution)/shard_map/ppermute | solution.py:47
  476.4 9.2 %collective-permute-done.50 = f32[384,512]{1,0:T(8,128)S(1)} collective-permute-done((f32[384,512]{1,0:T(8,128)S(1)}, f32[384,512]{1,0:T(8,128)S(1)}, u32[]{:S(2)}, u32[]{:S(2)}) %collective-permute-start.50) | collective-permute-done | bytes 786464 | tf_op jit(solution)/shard_map/ppermute | solution.py:47
  487.3 20.8 %collective-permute-done.34 = f32[512,512]{1,0:T(8,128)S(1)} collective-permute-done((f32[512,512]{1,0:T(8,128)S(1)}, f32[512,512]{1,0:T(8,128)S(1)}, u32[]{:S(2)}, u32[]{:S(2)}) %collective-permute-start.34) | collective-permute-done | bytes 1048608 | tf_op jit(solution)/shard_map/ppermute | solution.py:47
  510.0 16.9 %collective-permute-done.38 = f32[512,512]{1,0:T(8,128)S(1)} collective-permute-done((f32[512,512]{1,0:T(8,128)S(1)}, f32[512,512]{1,0:T(8,128)S(1)}, u32[]{:S(2)}, u32[]{:S(2)}) %collective-permute-start.38) | collective-permute-done | bytes 1048608 | tf_op jit(solution)/shard_map/ppermute | solution.py:47
  537.9 8.4 %collective-permute-done.52 = f32[512,256]{1,0:T(8,128)S(1)} collective-permute-done((f32[512,256]{1,0:T(8,128)}, f32[512,256]{1,0:T(8,128)S(1)}, u32[]{:S(2)}, u32[]{:S(2)}) %collective-permute-start.52) | collective-permute-done | bytes 524320 | tf_op jit(solution)/shard_map/ppermute | solution.py:119
  (330 shorter events, 231.0 us)
Async XLA Ops:
  0.6 58.4 %collective-permute-start = (f32[128,1024]{1,0:T(8,128)}, f32[128,1024]{1,0:T(8,128)}, u32[]{:S(2)}, u32[]{:S(2)}) collective-permute-start(f32[128,1024]{1,0:T(8,128)} %param.7), channel_id=1, source_target_pairs={{0,1},{1,0},{2,3},{3,2},{4,5},{5,4},{6,7},{7,6},{8,9},{9,8},{10,11... | collective-permute-start | bytes 1572872 | tf_op jit(solution)/shard_map/ppermute | solution.py:103
  6.7 130.9 %collective-permute-start.27 = (f32[256,1984]{0,1:T(8,128)}, f32[256,1984]{0,1:T(8,128)}, u32[]{:S(2)}, u32[]{:S(2)}) collective-permute-start(f32[256,1984]{0,1:T(8,128)} %slice.234), channel_id=1, source_target_pairs={{0,1},{1,0},{2,3},{3,2},{4,5},{5,4},{6,7},{7,6},{8,9},{9,8},{10,11... | collective-permute-start | bytes 6094856 | tf_op jit(solution)/shard_map/ppermute | solution.py:91
  19.6 52.5 %collective-permute-start.9 = (f32[256,1024]{1,0:T(8,128)}, f32[256,1024]{1,0:T(8,128)}, u32[]{:S(2)}, u32[]{:S(2)}) collective-permute-start(f32[256,1024]{1,0:T(8,128)} %slice_select_fusion.19), channel_id=1, source_target_pairs={{0,2},{2,0},{4,6},{6,4},{8,10},{10,8},{12,14},{14,12},{16,18},{18,... | collective-permute-start | bytes 3145736 | tf_op jit(solution)/shard_map/ppermute | solution.py:47
  25.0 162.1 %collective-permute-start.22 = (f32[384,1984]{0,1:T(8,128)}, f32[384,1984]{0,1:T(8,128)}, u32[]{:S(2)}, u32[]{:S(2)}) collective-permute-start(f32[384,1984]{0,1:T(8,128)} %get-tuple-element.33), channel_id=1, source_target_pairs={{0,1},{1,0},{2,3},{3,2},{4,5},{5,4},{6,7},{7,6},{8,9},{9,8},{10,11... | collective-permute-start | bytes 9142280 | tf_op jit(solution)/shard_map/ppermute | solution.py:91
  27.0 187.4 %collective-permute-start.17 = (f32[384,1984]{0,1:T(8,128)}, f32[384,1984]{0,1:T(8,128)}, u32[]{:S(2)}, u32[]{:S(2)}) collective-permute-start(f32[384,1984]{0,1:T(8,128)} %get-tuple-element.34), channel_id=1, source_target_pairs={{0,1},{1,0},{2,3},{3,2},{4,5},{5,4},{6,7},{7,6},{8,9},{9,8},{10,11... | collective-permute-start | bytes 9142280 | tf_op jit(solution)/shard_map/ppermute | solution.py:91
  61.0 39.4 %collective-permute-start.5 = (f32[128,1024]{1,0:T(8,128)S(1)}, f32[128,1024]{1,0:T(8,128)S(1)}, u32[]{:S(2)}, u32[]{:S(2)}) collective-permute-start(f32[128,1024]{1,0:T(8,128)S(1)} %get-tuple-element.61), channel_id=1, source_target_pairs={{16,0},{18,2},{20,4},{22,6},{24,8},{26,10},{28,12},{30,14},{17,1},... | collective-permute-start | bytes 1572872 | tf_op jit(solution)/shard_map/ppermute | solution.py:107
  113.4 125.1 %collective-permute-start.13 = (f32[768,1024]{1,0:T(8,128)}, f32[768,1024]{1,0:T(8,128)}, u32[]{:S(2)}, u32[]{:S(2)}) collective-permute-start(f32[768,1024]{1,0:T(8,128)} %slice_select_fusion), channel_id=1, source_target_pairs={{0,2},{2,0},{4,6},{6,4},{8,10},{10,8},{12,14},{14,12},{16,18},{18,... | collective-permute-start | bytes 9437192 | tf_op jit(solution)/shard_map/ppermute | solution.py:47
  137.5 44.3 %collective-permute-start.7 = (f32[2,128,1024]{2,1,0:T(8,128)}, f32[2,128,1024]{2,1,0:T(8,128)}, u32[]{:S(2)}, u32[]{:S(2)}) collective-permute-start(f32[2,128,1024]{2,1,0:T(8,128)} %pad_maximum_fusion.11), channel_id=1, source_target_pairs={{0,8},{2,10},{4,12},{6,14},{8,0},{10,2},{12,4},{14,6},{16,24},{18,... | collective-permute-start | bytes 3145736 | tf_op jit(solution)/shard_map/ppermute | solution.py:34
  163.2 46.9 %collective-permute-start.28 = (f32[256,1024]{1,0:T(8,128)}, f32[256,1024]{1,0:T(8,128)}, u32[]{:S(2)}, u32[]{:S(2)}) collective-permute-start(f32[256,1024]{1,0:T(8,128)} %slice_select_fusion.18), channel_id=1, source_target_pairs={{0,2},{2,0},{4,6},{6,4},{8,10},{10,8},{12,14},{14,12},{16,18},{18,... | collective-permute-start | bytes 3145736 | tf_op jit(solution)/shard_map/ppermute | solution.py:47
  181.8 76.1 %collective-permute-start.3 = (f32[2,2,128,1024]{3,2,1,0:T(8,128)}, f32[2,2,128,1024]{3,2,1,0:T(8,128)}, u32[]{:S(2)}, u32[]{:S(2)}) collective-permute-start(f32[2,2,128,1024]{3,2,1,0:T(8,128)} %pad_maximum_fusion.7), channel_id=1, source_target_pairs={{0,4},{2,6},{4,0},{6,2},{8,12},{10,14},{12,8},{14,10},{16,20},{18,... | collective-permute-start | bytes 6291464 | tf_op jit(solution)/shard_map/ppermute | solution.py:34
  187.1 79.8 %collective-permute-start.8 = (f32[2,2,128,1024]{3,2,1,0:T(8,128)}, f32[2,2,128,1024]{3,2,1,0:T(8,128)}, u32[]{:S(2)}, u32[]{:S(2)}) collective-permute-start(f32[2,2,128,1024]{3,2,1,0:T(8,128)} %pad_maximum_fusion.8), channel_id=1, source_target_pairs={{0,2},{2,0},{4,6},{6,4},{8,10},{10,8},{12,14},{14,12},{16,18},{18,... | collective-permute-start | bytes 6291464 | tf_op jit(solution)/shard_map/ppermute | solution.py:34
  210.1 50.6 %collective-permute-start.23 = (f32[384,1024]{1,0:T(8,128)}, f32[384,1024]{1,0:T(8,128)}, u32[]{:S(2)}, u32[]{:S(2)}) collective-permute-start(f32[384,1024]{1,0:T(8,128)} %slice_select_fusion.5), channel_id=1, source_target_pairs={{0,2},{2,0},{4,6},{6,4},{8,10},{10,8},{12,14},{14,12},{16,18},{18,... | collective-permute-start | bytes 4718600 | tf_op jit(solution)/shard_map/ppermute | solution.py:47
  260.6 102.7 %collective-permute-start.4 = (f32[2,2,2,128,1024]{4,3,2,1,0:T(8,128)S(1)}, f32[2,2,2,128,1024]{4,3,2,1,0:T(8,128)S(1)}, u32[]{:S(2)}, u32[]{:S(2)}) collective-permute-start(f32[2,2,2,128,1024]{4,3,2,1,0:T(8,128)S(1)} %pad_maximum_fusion.1), channel_id=1, source_target_pairs={{0,2},{2,0},{4,6},{6,4},{8,10},{10,8},{12,14},{14,12},{16,18},{18,... | collective-permute-start | bytes 12582920 | tf_op jit(solution)/shard_map/ppermute | solution.py:34
  264.0 46.3 %collective-permute-start.24 = (f32[384,512]{1,0:T(8,128)S(1)}, f32[384,512]{1,0:T(8,128)S(1)}, u32[]{:S(2)}, u32[]{:S(2)}) collective-permute-start(f32[384,512]{1,0:T(8,128)S(1)} %slice_select_fusion.20), channel_id=1, source_target_pairs={{0,4},{2,6},{4,0},{6,2},{8,12},{10,14},{12,8},{14,10},{16,20},{18,... | collective-permute-start | bytes 2359304 | tf_op jit(solution)/shard_map/ppermute | solution.py:47
  265.1 61.1 %collective-permute-start.19 = (f32[384,512]{1,0:T(8,128)S(1)}, f32[384,512]{1,0:T(8,128)S(1)}, u32[]{:S(2)}, u32[]{:S(2)}) collective-permute-start(f32[384,512]{1,0:T(8,128)S(1)} %slice_select_fusion.21), channel_id=1, source_target_pairs={{0,4},{2,6},{4,0},{6,2},{8,12},{10,14},{12,8},{14,10},{16,20},{18,... | collective-permute-start | bytes 2359304 | tf_op jit(solution)/shard_map/ppermute | solution.py:47
  415.9 112.7 %collective-permute-start.53 = (f32[512,256]{1,0:T(8,128)S(1)}, f32[512,256]{1,0:T(8,128)S(1)}, u32[]{:S(2)}, u32[]{:S(2)}) collective-permute-start(f32[512,256]{1,0:T(8,128)S(1)} %pad_maximum_fusion.21), channel_id=1, source_target_pairs={{0,1},{2,9},{4,5},{6,13},{8,3},{10,11},{12,7},{14,15},{17,16},{19,... | collective-permute-start | bytes 1572872 | tf_op jit(solution)/shard_map/ppermute | solution.py:119
  420.4 44.8 %collective-permute-start.33 = (f32[512,256]{1,0:T(8,128)S(1)}, f32[512,256]{1,0:T(8,128)S(1)}, u32[]{:S(2)}, u32[]{:S(2)}) collective-permute-start(f32[512,256]{1,0:T(8,128)S(1)} %pad_maximum_fusion.21), channel_id=1, source_target_pairs={{0,8},{2,10},{4,12},{6,14},{8,0},{10,2},{12,4},{14,6},{16,24},{18,... | collective-permute-start | bytes 1572872 | tf_op jit(solution)/shard_map/ppermute | solution.py:47
  426.0 44.8 %collective-permute-start.37 = (f32[512,256]{1,0:T(8,128)S(1)}, f32[512,256]{1,0:T(8,128)S(1)}, u32[]{:S(2)}, u32[]{:S(2)}) collective-permute-start(f32[512,256]{1,0:T(8,128)S(1)} %pad_maximum_fusion.22), channel_id=1, source_target_pairs={{0,8},{2,10},{4,12},{6,14},{8,0},{10,2},{12,4},{14,6},{16,24},{18,... | collective-permute-start | bytes 1572872 | tf_op jit(solution)/shard_map/ppermute | solution.py:47
  472.8 54.0 %collective-permute-start.38 = (f32[512,512]{1,0:T(8,128)S(1)}, f32[512,512]{1,0:T(8,128)S(1)}, u32[]{:S(2)}, u32[]{:S(2)}) collective-permute-start(f32[512,512]{1,0:T(8,128)S(1)} %pad_maximum_fusion.13), channel_id=1, source_target_pairs={{0,4},{2,6},{4,0},{6,2},{8,12},{10,14},{12,8},{14,10},{16,20},{18,... | collective-permute-start | bytes 3145736 | tf_op jit(solution)/shard_map/ppermute | solution.py:47
  474.7 55.3 %collective-permute-start.43 = (f32[256,1024]{1,0:T(8,128)}, f32[256,1024]{1,0:T(8,128)}, u32[]{:S(2)}, u32[]{:S(2)}) collective-permute-start(f32[256,1024]{1,0:T(8,128)} %pad_maximum_fusion.9), channel_id=1, source_target_pairs={{0,2},{2,0},{4,6},{6,4},{8,10},{10,8},{12,14},{14,12},{16,18},{18,... | collective-permute-start | bytes 3145736 | tf_op jit(solution)/shard_map/ppermute | solution.py:47
  485.7 64.9 %collective-permute-start.47 = (f32[384,1024]{1,0:T(8,128)}, f32[384,1024]{1,0:T(8,128)}, u32[]{:S(2)}, u32[]{:S(2)}) collective-permute-start(f32[384,1024]{1,0:T(8,128)} %pad_maximum_fusion.5), channel_id=1, source_target_pairs={{0,2},{2,0},{4,6},{6,4},{8,10},{10,8},{12,14},{14,12},{16,18},{18,... | collective-permute-start | bytes 4718600 | tf_op jit(solution)/shard_map/ppermute | solution.py:47
  508.1 43.8 %collective-permute-start.51 = (f32[384,1024]{1,0:T(8,128)}, f32[384,1024]{1,0:T(8,128)}, u32[]{:S(2)}, u32[]{:S(2)}) collective-permute-start(f32[384,1024]{1,0:T(8,128)} %pad_maximum_fusion.6), channel_id=1, source_target_pairs={{0,2},{2,0},{4,6},{6,4},{8,10},{10,8},{12,14},{14,12},{16,18},{18,... | collective-permute-start | bytes 4718600 | tf_op jit(solution)/shard_map/ppermute | solution.py:47
  526.9 42.6 %collective-permute-start.35 = (f32[512,1024]{1,0:T(8,128)}, f32[512,1024]{1,0:T(8,128)}, u32[]{:S(2)}, u32[]{:S(2)}) collective-permute-start(f32[512,1024]{1,0:T(8,128)} %pad_maximum_fusion.3), channel_id=1, source_target_pairs={{0,2},{2,0},{4,6},{6,4},{8,10},{10,8},{12,14},{14,12},{16,18},{18,... | collective-permute-start | bytes 6291464 | tf_op jit(solution)/shard_map/ppermute | solution.py:47
  529.5 40.0 %collective-permute-start.39 = (f32[512,1024]{1,0:T(8,128)}, f32[512,1024]{1,0:T(8,128)}, u32[]{:S(2)}, u32[]{:S(2)}) collective-permute-start(f32[512,1024]{1,0:T(8,128)} %pad_maximum_fusion.4), channel_id=1, source_target_pairs={{0,2},{2,0},{4,6},{6,4},{8,10},{10,8},{12,14},{14,12},{16,18},{18,... | collective-permute-start | bytes 6291464 | tf_op jit(solution)/shard_map/ppermute | solution.py:47
  (85 other events, 1476.4 us)
